TPU v7x, 32 devices: a whole 2x2x4 slice. The times are simulated.
32 devices in a mesh: dp: 8 (over z, y), head: 4 (over x, core).
Axes of the slice: x: 2, y: 2, z: 4, core: 2. Of those that a mesh axis runs over, the one named last changes fastest.
Arguments:
- tokens: bfloat16 [32768, 768], P(('dp', 'head')), may hold values from -6 to 6
- seq_lengths: int32 [64, 32], P('dp'), may hold values from 0 to 512, as said below
- qkv_weight: bfloat16 [2, 3, 768, 768], P(None, None, None, 'head'), may hold values from -0.21875 to 0.21875
- qv_bias: float32 [2, 2, 768], P(None, None, 'head'), may hold values from -3 to 3
- out_weight: bfloat16 [2, 768, 768], replicated, may hold values from -0.875 to 0.875
- out_bias: float32 [2, 768], replicated, may hold values from -3 to 3
- norm1_gain: float32 [2, 768], replicated, may hold values from 0.25 to 1.75
- norm1_shift: float32 [2, 768], replicated, may hold values from -3 to 3
- up_weight: bfloat16 [2, 768, 3072], replicated, may hold values from -0.21875 to 0.21875
- up_bias: float32 [2, 3072], replicated, may hold values from -3 to 3
- down_weight: bfloat16 [2, 3072, 768], replicated, may hold values from -0.109375 to 0.109375
- down_bias: float32 [2, 768], replicated, may hold values from -3 to 3
- norm2_gain: float32 [2, 768], replicated, may hold values from 0.25 to 1.75
- norm2_shift: float32 [2, 768], replicated, may hold values from -3 to 3
- out_grad: bfloat16 [32768, 768], P(('dp', 'head')), may hold values from -6 to 6
Outputs:
- out_state: bfloat16 [32768, 768], P(('dp', 'head'))
- input_grad: bfloat16 [32768, 768], P(('dp', 'head'))
- qkv_weight_grad: float32 [2, 3, 768, 768], P(None, None, 'dp', 'head')
- qv_bias_grad: float32 [2, 2, 768], replicated
- out_weight_grad: float32 [2, 768, 768], P(None, 'dp', 'head')
- out_bias_grad: float32 [2, 768], replicated
- norm1_gain_grad: float32 [2, 768], replicated
- norm1_shift_grad: float32 [2, 768], replicated
- up_weight_grad: float32 [2, 768, 3072], P(None, 'dp', 'head')
- up_bias_grad: float32 [2, 3072], replicated
- down_weight_grad: float32 [2, 3072, 768], P(None, 'head', 'dp')
- down_bias_grad: float32 [2, 768], replicated
- norm2_gain_grad: float32 [2, 768], replicated
- norm2_shift_grad: float32 [2, 768], replicated
Inputs may be any that keep to these rules, and one draw needn't show every extreme that they name: `seq_lengths`: each slot's row sums to 512; nonzero entries come first and zero entries mark no sequence; some slot holds a single sequence of 512 rows.
All inputs are finite; a program needn't handle non-finite values.
Results may differ from a plain program's by a relative error of at most 0.025.
Values may be sent and summed in bfloat16 or wider, within the bound.
No kernel may reach another device: no remote copies, remote signals or barrier semaphores. Data moves between devices by JAX's collectives and lax.ppermute only.
A program may use at most 256 MiB of HBM per device.

v0:
```python
import jax
import jax.numpy as jnp
from jax import lax
from jax.sharding import PartitionSpec as P

HD = 64
EPSILON = 1e-06


def norm_rows(values, gain, shift):
    centre = jnp.mean(values, axis=-1, keepdims=True)
    centred = values - centre
    spread = jnp.mean(centred * centred, axis=-1, keepdims=True)
    return centred * lax.rsqrt(spread + EPSILON) * gain + shift


def exact_gelu(values):
    return jax.nn.gelu(values, approximate=False)


def segment_ids(lengths, slot_rows):
    boundary = jnp.cumsum(lengths, axis=1)
    position = jnp.arange(slot_rows, dtype=jnp.int32)
    return jnp.sum((position[None, :, None] >= boundary[:, None, :]).astype(jnp.int32), axis=2)


def slot_scores(queries, keys_in, segments):
    scaling = queries.shape[-1] ** (-0.5)
    scores = (
        jnp.einsum("qhd,khd->hqk", queries, keys_in, preferred_element_type=jnp.float32) * scaling
    )
    inside = (segments[:, None] == segments[None, :])[None]
    return (scores, inside)


def slot_forward(packed):
    queries, keys_in, values_in, segments = packed
    scores, inside = slot_scores(queries, keys_in, segments)
    scores = jnp.where(inside, scores, -1e30)
    peak_score = jnp.max(scores, axis=-1, keepdims=True)
    weights = jnp.exp(scores - peak_score)
    denominator = jnp.sum(weights, axis=-1, keepdims=True)
    probability = (weights / denominator).astype(jnp.bfloat16)
    context = jnp.einsum("hqk,khd->qhd", probability, values_in, preferred_element_type=jnp.float32)
    return (context.astype(jnp.bfloat16), (peak_score + jnp.log(denominator))[..., 0])


def slot_backward(packed):
    queries, keys_in, values_in, grad_context, log_total, segments = packed
    scaling = queries.shape[-1] ** (-0.5)
    scores, inside = slot_scores(queries, keys_in, segments)
    probability = jnp.where(inside, jnp.exp(scores - log_total[..., None]), 0.0)
    grad_prob = jnp.einsum(
        "qhd,khd->hqk", grad_context, values_in, preferred_element_type=jnp.float32
    )
    shares = jnp.sum(probability * grad_prob, axis=-1, keepdims=True)
    grad_score = (probability * (grad_prob - shares)).astype(jnp.bfloat16)
    grad_query = (
        jnp.einsum("hqk,khd->qhd", grad_score, keys_in, preferred_element_type=jnp.float32)
        * scaling
    )
    grad_key = (
        jnp.einsum("hqk,qhd->khd", grad_score, queries, preferred_element_type=jnp.float32)
        * scaling
    )
    grad_value = jnp.einsum(
        "hqk,qhd->khd",
        probability.astype(jnp.bfloat16),
        grad_context,
        preferred_element_type=jnp.float32,
    )
    return (
        grad_query.astype(jnp.bfloat16),
        grad_key.astype(jnp.bfloat16),
        grad_value.astype(jnp.bfloat16),
    )


def on_device(
    tokens,
    seq_lengths,
    qkv_weight,
    qv_bias,
    out_weight,
    out_bias,
    norm1_gain,
    norm1_shift,
    up_weight,
    up_bias,
    down_weight,
    down_bias,
    norm2_gain,
    norm2_shift,
    out_grad,
):
    heads_count = lax.axis_size("head")
    head_index = lax.axis_index("head")
    local_rows, model_width = tokens.shape
    group_rows = local_rows * heads_count
    slots_here = seq_lengths.shape[0]
    slot_rows = group_rows // slots_here
    segments = segment_ids(seq_lengths, slot_rows)
    head_width = qkv_weight.shape[-1]
    local_heads = head_width // HD
    layers = qkv_weight.shape[0]
    qkv_shape = (slots_here, slot_rows, 3, local_heads, HD)
    hidden_state = tokens.astype(jnp.float32)
    kept_values = []
    for layer_index in range(layers):
        gathered = lax.all_gather(hidden_state.astype(jnp.bfloat16), "head", axis=0, tiled=True)
        projected = jnp.einsum(
            "rd,cde->rce", gathered, qkv_weight[layer_index], preferred_element_type=jnp.float32
        )
        bias_rows = jnp.stack(
            [
                qv_bias[layer_index, 0],
                jnp.zeros_like(qv_bias[layer_index, 0]),
                qv_bias[layer_index, 1],
            ]
        )
        projected = (projected + bias_rows[None]).astype(jnp.bfloat16)
        shaped = projected.reshape(qkv_shape)
        context, log_total = lax.map(
            slot_forward, (shaped[:, :, 0], shaped[:, :, 1], shaped[:, :, 2], segments)
        )
        context = context.reshape(group_rows, head_width)
        token_context = lax.all_to_all(context, "head", split_axis=0, concat_axis=1, tiled=True)
        attended = (
            jnp.dot(token_context, out_weight[layer_index], preferred_element_type=jnp.float32)
            + out_bias[layer_index]
        )
        first_sum = hidden_state + attended
        normed = norm_rows(first_sum, norm1_gain[layer_index], norm1_shift[layer_index])
        normed_low = normed.astype(jnp.bfloat16)
        ffn_rows = normed_low
        up_part = up_weight[layer_index]
        up_shift = up_bias[layer_index]
        down_part = down_weight[layer_index]
        before_gelu = jnp.dot(ffn_rows, up_part, preferred_element_type=jnp.float32) + up_shift
        activated = exact_gelu(before_gelu).astype(jnp.bfloat16)
        branch = jnp.dot(activated, down_part, preferred_element_type=jnp.float32)
        second_sum = normed + branch + down_bias[layer_index]
        hidden_state = norm_rows(second_sum, norm2_gain[layer_index], norm2_shift[layer_index])
        kept_values.append(
            (
                gathered,
                projected,
                log_total,
                token_context,
                first_sum,
                ffn_rows,
                up_part,
                down_part,
                before_gelu,
                activated,
                second_sum,
            )
        )
    out_state = hidden_state.astype(jnp.bfloat16)
    grad_state = out_grad.astype(jnp.float32)
    ffn_list, proj_list, attn_list, small_list, shift_list = ([], [], [], [], [])
    for layer_index in reversed(range(layers)):
        (
            gathered,
            projected,
            log_total,
            token_context,
            first_sum,
            ffn_rows,
            up_part,
            down_part,
            before_gelu,
            activated,
            second_sum,
        ) = kept_values[layer_index]
        pull_second = jax.vjp(
            norm_rows, second_sum, norm2_gain[layer_index], norm2_shift[layer_index]
        )[1]
        grad_second, grad_gain2, grad_shift2 = pull_second(grad_state)
        grad_branch = grad_second.astype(jnp.bfloat16)
        grad_down_shift = jnp.sum(grad_branch.astype(jnp.float32), axis=0)
        grad_down = jnp.einsum(
            "rd,rf->df", grad_branch, activated, preferred_element_type=jnp.float32
        )
        grad_act = jnp.einsum(
            "rd,fd->rf", grad_branch, down_part, preferred_element_type=jnp.float32
        )
        pull_gelu = jax.vjp(exact_gelu, before_gelu)[1]
        grad_pre = pull_gelu(grad_act)[0].astype(jnp.bfloat16)
        grad_up_shift = jnp.sum(grad_pre.astype(jnp.float32), axis=0)
        grad_up = jnp.einsum("rd,rf->df", ffn_rows, grad_pre, preferred_element_type=jnp.float32)
        grad_normed_low = jnp.einsum(
            "rf,df->rd", grad_pre, up_part, preferred_element_type=jnp.float32
        )
        grad_normed = grad_second + grad_normed_low
        pull_first = jax.vjp(
            norm_rows, first_sum, norm1_gain[layer_index], norm1_shift[layer_index]
        )[1]
        grad_first, grad_gain1, grad_shift1 = pull_first(grad_normed)
        grad_attended = grad_first.astype(jnp.bfloat16)
        grad_out_shift = jnp.sum(grad_attended.astype(jnp.float32), axis=0)
        grad_out = jnp.einsum(
            "rd,re->de", token_context, grad_attended, preferred_element_type=jnp.float32
        )
        grad_mixed = jnp.einsum(
            "re,de->rd", grad_attended, out_weight[layer_index], preferred_element_type=jnp.float32
        ).astype(jnp.bfloat16)
        grad_context = lax.all_to_all(grad_mixed, "head", split_axis=1, concat_axis=0, tiled=True)
        shaped = projected.reshape(qkv_shape)
        grad_query, grad_key, grad_value = lax.map(
            slot_backward,
            (
                shaped[:, :, 0],
                shaped[:, :, 1],
                shaped[:, :, 2],
                grad_context.reshape(slots_here, slot_rows, local_heads, HD),
                log_total,
                segments,
            ),
        )
        grad_proj = jnp.stack([grad_query, grad_key, grad_value], axis=2).reshape(
            group_rows, 3, head_width
        )
        grad_qkv = jnp.einsum(
            "rd,rce->cde", gathered, grad_proj, preferred_element_type=jnp.float32
        )
        bias_local = jnp.sum(grad_proj.astype(jnp.float32), axis=0)
        qv_local = jnp.stack([bias_local[0], bias_local[2]])
        qv_full = lax.dynamic_update_slice_in_dim(
            jnp.zeros((2, model_width), jnp.float32), qv_local, head_index * head_width, 1
        )
        layer_weights = qkv_weight[layer_index]
        grad_state = grad_first + lax.psum_scatter(
            jnp.einsum(
                "rce,cde->rd", grad_proj, layer_weights, preferred_element_type=jnp.float32
            ).astype(jnp.bfloat16),
            "head",
            scatter_dimension=0,
            tiled=True,
        ).astype(jnp.float32)
        ffn_list.append(jnp.stack([grad_up, grad_down]))
        proj_list.append(grad_out)
        attn_list.append(grad_qkv)
        small_list.append(
            jnp.concatenate(
                [
                    qv_full,
                    jnp.stack(
                        [
                            grad_out_shift,
                            grad_gain1,
                            grad_shift1,
                            grad_down_shift,
                            grad_gain2,
                            grad_shift2,
                        ]
                    ),
                ],
                axis=0,
            )
        )
        shift_list.append(grad_up_shift)
    input_grad = grad_state.astype(jnp.bfloat16)
    ffn_stack = jnp.stack(ffn_list[::-1])
    proj_stack = jnp.stack(proj_list[::-1])
    attn_stack = jnp.stack(attn_list[::-1])
    small_stack = jnp.stack(small_list[::-1])
    shift_stack = jnp.stack(shift_list[::-1])
    ffn_data, proj_data, attn_data = (
        lax.psum_scatter(
            ffn_stack.astype(jnp.bfloat16), "dp", scatter_dimension=2, tiled=True
        ).astype(jnp.float32),
        lax.psum_scatter(
            proj_stack.astype(jnp.bfloat16), "dp", scatter_dimension=1, tiled=True
        ).astype(jnp.float32),
        lax.psum_scatter(
            attn_stack.astype(jnp.bfloat16), "dp", scatter_dimension=2, tiled=True
        ).astype(jnp.float32),
    )
    ffn_head, proj_head = (
        lax.psum_scatter(
            ffn_data.astype(jnp.bfloat16), "head", scatter_dimension=3, tiled=True
        ).astype(jnp.float32),
        lax.psum_scatter(
            proj_data.astype(jnp.bfloat16), "head", scatter_dimension=2, tiled=True
        ).astype(jnp.float32),
    )
    small_sum, shift_sum = lax.psum((small_stack, shift_stack), ("dp", "head"))
    down_weight_grad = jnp.transpose(ffn_head[:, 1], (0, 2, 1))
    return (
        out_state,
        input_grad,
        attn_data,
        small_sum[:, 0:2],
        proj_head,
        small_sum[:, 2],
        small_sum[:, 3],
        small_sum[:, 4],
        ffn_head[:, 0],
        shift_sum,
        down_weight_grad,
        small_sum[:, 5],
        small_sum[:, 6],
        small_sum[:, 7],
    )


def solution(mesh):
    in_specs = (
        P(("dp", "head"), None),
        P("dp", None),
        P(None, None, None, "head"),
        P(None, None, "head"),
        P(),
        P(),
        P(),
        P(),
        P(),
        P(),
        P(),
        P(),
        P(),
        P(),
        P(("dp", "head"), None),
    )
    out_specs = (
        P(("dp", "head"), None),
        P(("dp", "head"), None),
        P(None, None, "dp", "head"),
        P(),
        P(None, "dp", "head"),
        P(),
        P(),
        P(),
        P(None, "dp", "head"),
        P(),
        P(None, "head", "dp"),
        P(),
        P(),
        P(),
    )
    return jax.shard_map(
        on_device, mesh=mesh, in_specs=in_specs, out_specs=out_specs, check_vma=False
    )
```

profile of v0, /device:TPU:0, one launch (start us, length us, event | category | flops | bytes accessed | tf_op | source)
XLA Modules:
  0.0 1406.1 jit_solution(3311266776964060774)
XLA Ops:
  12.9 45.8 %all-gather.3.cloned.1.call-done = bf16[4096,768]{1,0:T(8,128)(2,1)} async-done(((bf16[1024,768]{1,0:T(8,128)(2,1)}), bf16[4096,768]{1,0:T(8,128)(2,1)}) %all-gather.3.cloned.1.call-update) | async-done | bytes 6291472 | tf_op jit(solution)/shard_map/all_gather | solution.py:110
  58.7 6.0 fusion.216
  73.9 35.4 %while.52 = (s32[]{:T(128)}, bf16[8,512,3,64]{1,3,2,0:T(8,128)(2,1)}, f32[8,3,512]{2,1,0:T(4,128)S(1)}, bf16[8,512,3,64]{1,3,2,0:T(8,128)(2,1)}, s32[8,512]{1,0:...) while((s32[]{:T(128)}, ...), condition=%wide.region_5.6_spmd, body=%wide.region_2.5_spmd.sunk | while | flops 211122688 | bytes 11335773 | solution.py:123
  109.2 4.6 copy.159
  113.8 13.7 all_to_all.52
  139.1 15.2 %all-to-all-done = bf16[4,1024,192]{1,2,0:T(8,128)(2,1)S(1)} async-done(((bf16[4,1024,192]{1,2,0:T(8,128)(2,1)}), bf16[4,1024,192]{1,2,0:T(8,128)(2,1)S(1)}, u32[]{:S(2)}, u32[]{:S(2)}) %all-to-all-start) | async-done | bytes 1572896 | tf_op jit(solution)/shard_map/all_to_all | solution.py:127
  154.4 4.0 fusion.212
  158.9 38.8 %multiply_convert_fusion.3 = (bf16[1024,3072]{1,0:T(8,128)(2,1)}, f32[1024,3072]{1,0:T(8,128)}, f32[1024,3072]{1,0:T(8,128)}) fusion(f32[3072]{0:T(1024)S(1)} %bitcast.494, bf16[2,768,3072]{2,1,0:T(8,128)(2,1)} %param.31, f32[1024,768]{0,1:T(8,128)S(1)} %get-tuple-element.478, f32[768]{0:T(1024)S(1)} %get-tuple-element.347, ...), kind=kOutput, calls=%fused_computation.148 | convolution fusion | flops 5043388416 | bytes 39348224 | tf_op jit(solution)/shard_map/dot_general | solution.py:139
  197.8 8.6 fusion.213
  208.6 46.5 %all-gather.5.cloned.1.call-done = bf16[4096,768]{0,1:T(8,128)(2,1)} async-done(((bf16[1024,768]{0,1:T(8,128)(2,1)}), bf16[4096,768]{0,1:T(8,128)(2,1)}) %all-gather.5.cloned.1.call-update) | async-done | bytes 6291472 | tf_op jit(solution)/shard_map/all_gather | solution.py:110
  255.2 6.6 fusion.217
  273.1 43.5 %while.53 = (s32[]{:T(128)}, bf16[8,512,3,64]{1,3,2,0:T(8,128)(2,1)}, f32[8,3,512]{2,1,0:T(4,128)S(1)}, bf16[8,512,3,64]{1,3,2,0:T(8,128)(2,1)}, s32[8,512]{1,0:...) while((s32[]{:T(128)}, ...), condition=%wide.region_13.14_spmd, body=%wide.region_10.13_spmd.sunk | while | flops 211122688 | bytes 11335773 | solution.py:123
  327.0 4.6 all-to-all-start.1
  334.3 17.5 %all-to-all-done.1 = bf16[4,1024,192]{1,2,0:T(8,128)(2,1)} async-done(((bf16[4,1024,192]{1,2,0:T(8,128)(2,1)}), bf16[4,1024,192]{1,2,0:T(8,128)(2,1)}, u32[]{:S(2)}, u32[]{:S(2)}) %all-to-all-start.1) | async-done | bytes 1572896 | tf_op jit(solution)/shard_map/all_to_all | solution.py:127
  356.5 38.4 %multiply_convert_fusion.2 = (bf16[1024,3072]{1,0:T(8,128)(2,1)}, f32[1024,3072]{1,0:T(8,128)}, f32[1024,3072]{1,0:T(8,128)}) fusion(f32[3072]{0:T(1024)S(1)} %bitcast.497, bf16[2,768,3072]{2,1,0:T(8,128)(2,1)} %param.31, f32[1024,768]{0,1:T(8,128)S(1)} %get-tuple-element.483, f32[768]{0:T(1024)S(1)} %copy-done.73, f32[768]{0:T(1024)S(1)} %copy-done.52, ...), kind=kOutput, calls=%fused_computation.135 | convolution fusion | flops 5043388416 | bytes 39348224 | tf_op jit(solution)/shard_map/dot_general | solution.py:139
  395.0 8.9 fusion.215
  411.1 18.2 %convert_reduce_fusion = (f32[3072]{0:T(1024)}, bf16[1024,3072]{1,0:T(8,128)(2,1)}) fusion(f32[1024,3072]{1,0:T(8,128)} %get-tuple-element.435, bf16[1024,768]{0,1:T(8,128)(2,1)S(1)} %get-tuple-element.425, bf16[2,3072,768]{2,1,0:T(8,128)(2,1)} %param.33, f32[1024,3072]{1,0:T(8,128)} %get-tuple-element.484, f32[3072]{0:T(1024)S(1)} %bitcast.498), kind=kOutput, calls=%fused_computation.131 | convolution fusion | flops 4885312512 | bytes 37773312 | tf_op jit(solution)/shard_map/rd,fd->rf/dot_general | solution.py:185
  429.4 11.7 multiply_reduce_fusion.2
  451.5 20.0 %all-to-all-done.2 = bf16[1024,4,192]{0,2,1:T(8,128)(2,1)S(1)} async-done(((bf16[1024,4,192]{0,2,1:T(8,128)(2,1)}), bf16[1024,4,192]{0,2,1:T(8,128)(2,1)S(1)}, u32[]{:S(2)}, u32[]{:S(2)}) %all-to-all-start.2) | async-done | bytes 1572896 | tf_op jit(solution)/shard_map/all_to_all | solution.py:208
  479.6 88.1 %while.54 = (s32[]{:T(128)}, bf16[8,512,3,64]{1,3,2,0:T(8,128)(2,1)S(1)}, bf16[8,512,3,64]{1,3,2,0:T(8,128)(2,1)}, bf16[8,512,3,64]{1,3,2,0:T(8,128)(2,1)}, bf16...) while((s32[]{:T(128)}, ...), condition=%wide.region_24.25_spmd, body=%wide.region_22.24_spmd.sunk | while | flops 511146496 | bytes 26125428 | solution.py:210
  583.9 9.5 bitcast_convert_fusion.1
  594.8 4.0 fusion.172
  598.8 11.7 fusion.140
  610.5 41.4 %reduce-scatter.12.cloned.1.call-done = bf16[1024,768]{0,1:T(8,128)(2,1)} async-done(((bf16[4096,768]{0,1:T(8,128)(2,1)}), bf16[1024,768]{0,1:T(8,128)(2,1)}) %reduce-scatter.12.cloned.1.call-update) | async-done | bytes 1572880 | tf_op jit(solution)/shard_map/reduce_scatter | solution.py:233
  651.9 3.9 multiply_reduce_fusion.3
  659.1 18.5 %convert_reduce_fusion.1 = (f32[3072]{0:T(1024)S(1)}, bf16[1024,3072]{1,0:T(8,128)(2,1)}) fusion(f32[1024,3072]{1,0:T(8,128)} %get-tuple-element.437, bf16[1024,768]{0,1:T(8,128)(2,1)} %get-tuple-element.421, bf16[2,3072,768]{2,1,0:T(8,128)(2,1)} %param.33, f32[1024,3072]{1,0:T(8,128)} %get-tuple-element.479, f32[3072]{0:T(1024)S(1)} %bitcast.495), kind=kOutput, calls=%fused_computation.132 | convolution fusion | flops 4885312512 | bytes 37773312 | tf_op jit(solution)/shard_map/rd,fd->rf/dot_general | solution.py:185
  677.7 9.9 multiply_reduce_fusion.4
  693.2 9.0 fusion.141
  702.3 8.4 maximum_bitcast_fusion.1
  710.6 9.3 fusion.139
  719.9 9.8 fusion.138
  729.7 8.3 maximum_bitcast_fusion
  738.1 16.7 %pad_maximum_fusion = bf16[2,2,768,3072]{3,2,1,0:T(8,128)(2,1)} fusion(bf16[1,2,768,3072]{3,2,1,0:T(8,128)(2,1)} %maximum_bitcast_fusion.1, bf16[1,2,768,3072]{3,2,1,0:T(8,128)(2,1)} %maximum_bitcast_fusion), kind=kLoop, calls=%fused_computation.126 | loop fusion | flops 9437184 | bytes 37748736 | tf_op jit(solution)/shard_map/stack | solution.py:264
  758.9 4.3 convolution_convert_fusion.4
  763.2 4.3 all-to-all-start.3
  768.0 9.0 fusion.173
  777.7 10.0 all-to-all-done.3
  802.2 101.9 %while.55 = (s32[]{:T(128)}, bf16[8,512,3,64]{1,3,2,0:T(8,128)(2,1)}, bf16[8,512,3,64]{1,3,2,0:T(8,128)(2,1)}, bf16[8,512,3,64]{1,3,2,0:T(8,128)(2,1)}, bf16[8,5...) while((s32[]{:T(128)}, ...), condition=%wide.region_32.33_spmd, body=%wide.region_30.32_spmd.sunk | while | flops 511146496 | bytes 26125428 | solution.py:210
  932.2 8.1 fusion.176
  941.8 5.9 copy.207
  947.7 6.9 reshape.411
  957.0 9.7 bitcast_convert_fusion
  966.8 112.1 %reduce-scatter.18.cloned.1.call-done = bf16[2,2,96,3072]{3,2,1,0:T(8,128)(2,1)} async-done(((bf16[2,2,768,3072]{3,2,1,0:T(8,128)(2,1)}), bf16[2,2,96,3072]{3,2,1,0:T(8,128)(2,1)}) %reduce-scatter.18.cloned.1.call-update) | async-done | bytes 2359312 | tf_op jit(solution)/shard_map/reduce_scatter | solution.py:270
  1081.6 122.8 %all-reduce.3.cloned.1.call-done = (f32[2,8,768]{2,0,1:T(2,128)}, f32[2,3072]{1,0:T(2,128)}) async-done(((f32[2,8,768]{2,0,1:T(2,128)}, f32[2,3072]{1,0:T(2,128)}), (f32[2,8,768]{2,0,1:T(2,128)}, f32[2,3072]{1,0:T(2,128)})) %all-reduce.3.cloned.1.call-update) | async-done | bytes 73744 | tf_op jit(solution)/shard_map/psum | solution.py:288
  1207.1 69.8 %reduce-scatter.22.cloned.1.call-done = bf16[96,1152]{1,0:T(8,128)(2,1)} async-done(((bf16[768,1152]{1,0:T(8,128)(2,1)}), bf16[96,1152]{1,0:T(8,128)(2,1)}) %reduce-scatter.22.cloned.1.call-update) | async-done | bytes 221200
  1281.1 18.6 %reduce-scatter.24.cloned.1.call-done = bf16[192,192]{1,0:T(8,128)(2,1)} async-done(((bf16[768,192]{1,0:T(8,128)(2,1)}), bf16[192,192]{1,0:T(8,128)(2,1)}) %reduce-scatter.24.cloned.1.call-update) | async-done | bytes 73744
  1301.4 59.1 %reduce-scatter.14.cloned.1.call-done = bf16[1024,768]{0,1:T(8,128)(2,1)} async-done(((bf16[4096,768]{0,1:T(8,128)(2,1)}), bf16[1024,768]{0,1:T(8,128)(2,1)}) %reduce-scatter.14.cloned.1.call-update) | async-done | bytes 1572880 | tf_op jit(solution)/shard_map/reduce_scatter | solution.py:233
  1366.3 29.9 %reduce-scatter.20.cloned.1.call-done = bf16[2,2,96,768]{3,2,1,0:T(8,128)(2,1)} async-done(((bf16[2,2,96,3072]{3,2,1,0:T(8,128)(2,1)}), bf16[2,2,96,768]{3,2,1,0:T(8,128)(2,1)}) %reduce-scatter.20.cloned.1.call-update) | async-done | bytes 589840 | tf_op jit(solution)/shard_map/reduce_scatter | solution.py:281
  (575 shorter events, 449.4 us)
Async XLA Ops:
  7.2 51.5 %all-gather.3.cloned.1.call-start = ((), (), s32[]{:S(2)}) async-start(), calls=%async_computation.11 | async-start | bytes 7864320 | tf_op jit(solution)/shard_map/all_gather | solution.py:110
  109.2 18.3 %copy-start.6 = (bf16[8,512,3,64]{1,3,2,0:T(8,128)(2,1)}, bf16[8,512,3,64]{1,3,2,0:T(8,128)(2,1)S(1)}, u32[]{:S(2)}) copy-start(bf16[8,512,3,64]{1,3,2,0:T(8,128)(2,1)S(1)} %get-tuple-element.867) | copy-start | bytes 4718596
  109.2 18.3 %copy-start.31 = (f32[8,3,512]{2,1,0:T(4,128)}, f32[8,3,512]{2,1,0:T(4,128)S(1)}, u32[]{:S(2)}) copy-start(f32[8,3,512]{2,1,0:T(4,128)S(1)} %get-tuple-element.811) | copy-start | bytes 147460
  130.6 23.8 %all-to-all-start = ((bf16[4,1024,192]{1,2,0:T(8,128)(2,1)}), bf16[4,1024,192]{1,2,0:T(8,128)(2,1)S(1)}, u32[]{:S(2)}, u32[]{:S(2)}) async-start(bf16[4,1024,192]{1,2,0:T(8,128)(2,1)} %copy.160), calls=%async_computation | async-start | bytes 3145728 | tf_op jit(solution)/shard_map/all_to_all | solution.py:127
  134.3 120.8 %all-gather.5.cloned.1.call-start = ((), (), s32[]{:S(2)}) async-start(), calls=%async_computation.12 | async-start | bytes 7864320 | tf_op jit(solution)/shard_map/all_gather | solution.py:110
  137.9 59.8 %copy-start.50 = (f32[768]{0:T(1024)}, f32[768]{0:T(1024)S(1)}, u32[]{:S(2)}) copy-start(f32[768]{0:T(1024)S(1)} %get-tuple-element.495) | copy-start | bytes 9220
  137.9 59.8 %copy-start.71 = (f32[768]{0:T(1024)}, f32[768]{0:T(1024)S(1)}, u32[]{:S(2)}) copy-start(f32[768]{0:T(1024)S(1)} %get-tuple-element.347) | copy-start | bytes 9220
  138.5 213.3 %copy-start.35 = (f32[768]{0:T(1024)}, f32[768]{0:T(1024)S(1)}, u32[]{:S(2)}) copy-start(f32[768]{0:T(1024)S(1)} %get-tuple-element.497) | copy-start | bytes 9220
  139.1 19.7 %copy-start.61 = (f32[1,3072]{1,0:T(1,128)}, f32[1,3072]{1,0:T(1,128)S(1)}, u32[]{:S(2)}) copy-start(f32[1,3072]{1,0:T(1,128)S(1)} %get-tuple-element.464) | copy-start | bytes 36868
  154.4 43.4 %slice-start = ((s8[9437184]{0:T(1024)(128)(4,1)}), s8[4194304]{0:T(1024)(128)(4,1)S(1)}, s32[]{:S(2)}) async-start(s8[9437184]{0:T(1024)(128)(4,1)} %bitcast.500), calls=%async_computation.21 | async-start | bytes 8388608
  158.4 39.3 %copy-start.7 = (f32[1024,768]{0,1:T(8,128)}, f32[1024,768]{0,1:T(8,128)S(1)}, u32[]{:S(2)}) copy-start(f32[1024,768]{0,1:T(8,128)S(1)} %get-tuple-element.478) | copy-start | bytes 9437188
  158.4 39.3 %copy-start.40 = (f32[1024]{0:T(1024)}, f32[1024]{0:T(1024)S(1)}, u32[]{:S(2)}) copy-start(f32[1024]{0:T(1024)S(1)} %broadcast_multiply_fusion.3) | copy-start | bytes 12292
  158.8 38.8 %copy-start.42 = (f32[1024]{0:T(1024)}, f32[1024]{0:T(1024)S(1)}, u32[]{:S(2)}) copy-start(f32[1024]{0:T(1024)S(1)} %multiply_reduce_fusion.11) | copy-start | bytes 12292
  158.9 38.9 %copy-start.57 = (f32[1024]{0:T(1024)}, f32[1024]{0:T(1024)S(1)}, u32[]{:S(2)}) copy-start(f32[1024]{0:T(1024)S(1)} %fusion.189) | copy-start | bytes 12292
  158.9 38.9 %slice-start.1 = ((s8[9437184]{0:T(1024)(128)(4,1)}), s8[4194304]{0:T(1024)(128)(4,1)S(1)}, s32[]{:S(2)}) async-start(s8[9437184]{0:T(1024)(128)(4,1)} %bitcast.500), calls=%async_computation.22 | async-start | bytes 8388608
  158.9 38.9 %slice-start.2 = ((s8[9437184]{0:T(1024)(128)(4,1)}), s8[1048576]{0:T(1024)(128)(4,1)S(1)}, s32[]{:S(2)}) async-start(s8[9437184]{0:T(1024)(128)(4,1)} %bitcast.500), calls=%async_computation.23 | async-start | bytes 2097152
  206.4 145.4 %copy-start = (f32[1024,768]{0,1:T(8,128)}, f32[1024,768]{0,1:T(8,128)S(1)}, u32[]{:S(2)}) copy-start(f32[1024,768]{0,1:T(8,128)S(1)} %get-tuple-element.481) | copy-start | bytes 9437188
  206.4 145.4 %copy-start.33 = (f32[1024]{0:T(1024)}, f32[1024]{0:T(1024)S(1)}, u32[]{:S(2)}) copy-start(f32[1024]{0:T(1024)S(1)} %broadcast_multiply_fusion.2) | copy-start | bytes 12292
  206.8 145.0 %copy-start.37 = (f32[1024]{0:T(1024)}, f32[1024]{0:T(1024)S(1)}, u32[]{:S(2)}) copy-start(f32[1024]{0:T(1024)S(1)} %fusion.190) | copy-start | bytes 12292
  327.0 24.8 %copy-start.75 = (f32[768]{0:T(1024)S(1)}, f32[768]{0:T(1024)}, u32[]{:S(2)}) copy-start(f32[768]{0:T(1024)} %get-tuple-element.348) | copy-start | bytes 9220
  327.0 24.8 %all-to-all-start.1 = ((bf16[4,1024,192]{1,2,0:T(8,128)(2,1)}), bf16[4,1024,192]{1,2,0:T(8,128)(2,1)}, u32[]{:S(2)}, u32[]{:S(2)}) async-start(bf16[4,1024,192]{1,2,0:T(8,128)(2,1)} %copy.166), calls=%async_computation.1 | async-start | bytes 3145728 | tf_op jit(solution)/shard_map/all_to_all | solution.py:127
  351.8 43.1 %slice-start.3 = ((s8[9437184]{0:T(1024)(128)(4,1)}), s8[4194304]{0:T(1024)(128)(4,1)S(1)}, s32[]{:S(2)}) async-start(s8[9437184]{0:T(1024)(128)(4,1)} %bitcast.502), calls=%async_computation.24 | async-start | bytes 8388608
  355.7 39.3 %copy-start.10 = (f32[1024,768]{0,1:T(8,128)}, f32[1024,768]{0,1:T(8,128)S(1)}, u32[]{:S(2)}) copy-start(f32[1024,768]{0,1:T(8,128)S(1)} %get-tuple-element.483) | copy-start | bytes 9437188
  356.1 38.8 %copy-start.46 = (f32[1024]{0:T(1024)}, f32[1024]{0:T(1024)S(1)}, u32[]{:S(2)}) copy-start(f32[1024]{0:T(1024)S(1)} %multiply_reduce_fusion.9) | copy-start | bytes 12292
  356.5 38.5 %copy-start.74 = (f32[768]{0:T(1024)S(1)}, f32[768]{0:T(1024)}, u32[]{:S(2)}) copy-start(f32[768]{0:T(1024)} %get-tuple-element.342) | copy-start | bytes 9220
  356.5 38.5 %slice-start.4 = ((s8[9437184]{0:T(1024)(128)(4,1)}), s8[4194304]{0:T(1024)(128)(4,1)S(1)}, s32[]{:S(2)}) async-start(s8[9437184]{0:T(1024)(128)(4,1)} %bitcast.502), calls=%async_computation.25 | async-start | bytes 8388608
  356.5 38.5 %slice-start.5 = ((s8[9437184]{0:T(1024)(128)(4,1)}), s8[1048576]{0:T(1024)(128)(4,1)S(1)}, s32[]{:S(2)}) async-start(s8[9437184]{0:T(1024)(128)(4,1)} %bitcast.502), calls=%async_computation.26 | async-start | bytes 2097152
  447.9 23.6 %all-to-all-start.2 = ((bf16[1024,4,192]{0,2,1:T(8,128)(2,1)}), bf16[1024,4,192]{0,2,1:T(8,128)(2,1)S(1)}, u32[]{:S(2)}, u32[]{:S(2)}) async-start(bf16[1024,4,192]{0,2,1:T(8,128)(2,1)} %bitcast.68), calls=%async_computation.2 | async-start | bytes 3145728 | tf_op jit(solution)/shard_map/all_to_all | solution.py:208
  451.4 200.5 %reduce-scatter.12.cloned.1.call-start = ((), (), s32[]{:S(2)}) async-start(), calls=%async_computation.13 | async-start | bytes 7864320 | tf_op jit(solution)/shard_map/reduce_scatter | solution.py:233
  593.4 361.3 %reduce-scatter.16.cloned.1.call-start = ((), (), s32[]{:S(2)}) async-start(), calls=%async_computation.15 | async-start | bytes 2654208 | tf_op jit(solution)/shard_map/reduce_scatter | solution.py:273
  598.8 53.1 %copy-start.1 = (f32[1024,768]{0,1:T(8,128)S(1)}, f32[1024,768]{0,1:T(8,128)}, u32[]{:S(2)}) copy-start(f32[1024,768]{0,1:T(8,128)} %copy-done) | copy-start | bytes 9437188
  598.8 53.1 %copy-start.34 = (f32[1024]{0:T(1024)S(1)}, f32[1024]{0:T(1024)}, u32[]{:S(2)}) copy-start(f32[1024]{0:T(1024)} %copy-done.33) | copy-start | bytes 12292
  598.8 53.1 %copy-start.36 = (f32[768]{0:T(1024)S(1)}, f32[768]{0:T(1024)}, u32[]{:S(2)}) copy-start(f32[768]{0:T(1024)} %copy-done.35) | copy-start | bytes 9220
  598.8 53.1 %copy-start.38 = (f32[1024]{0:T(1024)S(1)}, f32[1024]{0:T(1024)}, u32[]{:S(2)}) copy-start(f32[1024]{0:T(1024)} %copy-done.37) | copy-start | bytes 12292
  610.5 45.3 %copy-start.45 = (f32[1024]{0:T(1024)S(1)}, f32[1024]{0:T(1024)}, u32[]{:S(2)}) copy-start(f32[1024]{0:T(1024)} %copy-done.44) | copy-start | bytes 12292
  659.1 18.5 %copy-start.8 = (f32[1024,768]{0,1:T(8,128)S(1)}, f32[1024,768]{0,1:T(8,128)}, u32[]{:S(2)}) copy-start(f32[1024,768]{0,1:T(8,128)} %copy-done.7) | copy-start | bytes 9437188
  659.1 18.5 %copy-start.14 = (f32[1024,768]{0,1:T(8,128)S(1)}, f32[1024,768]{0,1:T(8,128)}, u32[]{:S(2)}) copy-start(f32[1024,768]{0,1:T(8,128)} %copy-done.13) | copy-start | bytes 9437188
  659.1 18.5 %copy-start.41 = (f32[1024]{0:T(1024)S(1)}, f32[1024]{0:T(1024)}, u32[]{:S(2)}) copy-start(f32[1024]{0:T(1024)} %copy-done.40) | copy-start | bytes 12292
  659.1 18.6 %copy-start.51 = (f32[768]{0:T(1024)S(1)}, f32[768]{0:T(1024)}, u32[]{:S(2)}) copy-start(f32[768]{0:T(1024)} %copy-done.50) | copy-start | bytes 9220
  659.1 18.6 %copy-start.58 = (f32[1024]{0:T(1024)S(1)}, f32[1024]{0:T(1024)}, u32[]{:S(2)}) copy-start(f32[1024]{0:T(1024)} %copy-done.57) | copy-start | bytes 12292
  693.2 385.8 %reduce-scatter.18.cloned.1.call-start = ((), (), s32[]{:S(2)}) async-start(), calls=%async_computation.16 | async-start | bytes 21233664 | tf_op jit(solution)/shard_map/reduce_scatter | solution.py:270
  763.2 24.5 %all-to-all-start.3 = ((bf16[1024,4,192]{0,2,1:T(8,128)(2,1)}), bf16[1024,4,192]{0,2,1:T(8,128)(2,1)}, u32[]{:S(2)}, u32[]{:S(2)}) async-start(bf16[1024,4,192]{0,2,1:T(8,128)(2,1)} %bitcast.483), calls=%async_computation.4 | async-start | bytes 3145728 | tf_op jit(solution)/shard_map/all_to_all | solution.py:208
  767.6 436.8 %all-reduce.3.cloned.1.call-start = ((), (), s32[]{:S(2)}) async-start(), calls=%async_computation.20 | async-start | bytes 147456 | tf_op jit(solution)/shard_map/psum | solution.py:288
  932.0 344.8 %reduce-scatter.22.cloned.1.call-start = ((), (), s32[]{:S(2)}) async-start(), calls=%async_computation.18 | async-start | bytes 1990656
  954.6 345.0 %reduce-scatter.24.cloned.1.call-start = ((), (), s32[]{:S(2)}) async-start(), calls=%async_computation.19 | async-start | bytes 491520
  957.0 403.6 %reduce-scatter.14.cloned.1.call-start = ((), (), s32[]{:S(2)}) async-start(), calls=%async_computation.14 | async-start | bytes 7864320 | tf_op jit(solution)/shard_map/reduce_scatter | solution.py:233
  966.8 429.4 %reduce-scatter.20.cloned.1.call-start = ((), (), s32[]{:S(2)}) async-start(), calls=%async_computation.17 | async-start | bytes 2949120 | tf_op jit(solution)/shard_map/reduce_scatter | solution.py:281
  1363.7 34.8 %copy-start.49 = (f32[2,3072]{1,0:T(2,128)S(1)}, f32[2,3072]{1,0:T(2,128)}, u32[]{:S(2)}) copy-start(f32[2,3072]{1,0:T(2,128)} %get-tuple-element.846) | copy-start | bytes 73732
  (51 other events, 261.4 us)
Sparse Core Ops, SparseCore 0:
  9.6 49.0 all-gather.2
  208.7 46.3 all-gather.4
  593.5 58.3 reduce-scatter.11
  693.3 69.0 reduce-scatter.15
  766.6 312.3 reduce-scatter.17
  1086.6 117.7 all-reduce.2
  1208.2 68.5 reduce-scatter.21
  1279.9 19.7 reduce-scatter.23
  1302.2 58.3 reduce-scatter.13
  1363.1 33.0 reduce-scatter.19
where the time goes:
time: 1420 us; the launch traced here: 1410 us
  waiting for transfers between devices  610 us (43%)
  matrix products  475 us (33%)
  local copies, waits for them, and re-layouts  185 us (13%)
  other arithmetic  102 us (7%)
  starting transfers between devices  17.2 us (1%)
  between operations  15.7 us (1%)
    psum x1, waiting for transfers between devices, on_device(): small_sum, shift_sum = lax.psum((small_stack, shift_stack), ('dp', 'head'))  123 us
    reduce_scatter x1, waiting for transfers between devices, on_device(): lax.psum_scatter(ffn_stack.astype(jnp.bfloat16), 'dp', scatter_dimension=...  112 us
    reduce_scatter x2, waiting for transfers between devices, on_device(): lax.psum_scatter(jnp.einsum('rce,cde->rd', grad_proj, layer_weights, pref...  101 us
    all_gather x2, waiting for transfers between devices, on_device(): lax.all_gather(hidden_state.astype(jnp.bfloat16), 'head', axis=0, tiled=T...  92.3 us
    unnamed x12, waiting for transfers between devices  89.2 us
    dot_general x2, matrix products, on_device(): jnp.dot(ffn_rows, up_part, preferred_element_type=jnp.float32) + up_shift  77.2 us
    unnamed x195, local copies, waits for them, and re-layouts  57.6 us
    dot_general x32, matrix products, slot_scores(): jnp.einsum('qhd,khd->hqk', queries, keys_in, preferred_element_type=jnp.f...  55.1 us
  transfers between devices with their start and end apart: 14, of which 13 were waited for; matrix products, arithmetic and copies ran while one was open for 21% of the time, Pallas kernels for 0%

commit v1 on v0

--- a/solution.py
+++ b/solution.py
@@ -124,7 +124,12 @@
             slot_forward, (shaped[:, :, 0], shaped[:, :, 1], shaped[:, :, 2], segments)
         )
         context = context.reshape(group_rows, head_width)
-        token_context = lax.all_to_all(context, "head", split_axis=0, concat_axis=1, tiled=True)
+        token_context = jnp.concatenate(
+            lax.all_to_all(
+                jnp.stack(jnp.split(context, lax.axis_size("head"), axis=0)), "head", 0, 0
+            ),
+            axis=1,
+        )
         attended = (
             jnp.dot(token_context, out_weight[layer_index], preferred_element_type=jnp.float32)
             + out_bias[layer_index]

time: 1420 us -> 1420 us (level)
    all_to_all x4 -> x0, local copies, waits for them, and re-layouts: 23.6 us -> none  [on_device(): lax.all_to_all(context, 'head', split_axis=0, concat_axis=1, tiled=True)]
    split x0 -> x10, local copies, waits for them, and re-layouts: none -> 17.6 us  [on_device(): jnp.split(context, lax.axis_size('head'), axis=0)]
    unnamed x195 -> x209, local copies, waits for them, and re-layouts: 57.6 us -> 59 us
where the time goes in v1:
time: 1420 us; the launch traced here: 1410 us
  waiting for transfers between devices  609 us (43%)
  matrix products  477 us (34%)
  local copies, waits for them, and re-layouts  184 us (13%)
  other arithmetic  107 us (8%)
  starting transfers between devices  17 us (1%)
  between operations  15.7 us (1%)
    psum x1, waiting for transfers between devices, on_device(): small_sum, shift_sum = lax.psum((small_stack, shift_stack), ('dp', 'head'))  123 us
    reduce_scatter x1, waiting for transfers between devices, on_device(): lax.psum_scatter(ffn_stack.astype(jnp.bfloat16), 'dp', scatter_dimension=...  112 us
    reduce_scatter x2, waiting for transfers between devices, on_device(): lax.psum_scatter(jnp.einsum('rce,cde->rd', grad_proj, layer_weights, pref...  100 us
    all_gather x2, waiting for transfers between devices, on_device(): lax.all_gather(hidden_state.astype(jnp.bfloat16), 'head', axis=0, tiled=T...  92.3 us
    unnamed x12, waiting for transfers between devices  89.2 us
    dot_general x2, matrix products, on_device(): jnp.dot(ffn_rows, up_part, preferred_element_type=jnp.float32) + up_shift  78.1 us
    unnamed x209, local copies, waits for them, and re-layouts  59 us
    dot_general x32, matrix products, slot_scores(): jnp.einsum('qhd,khd->hqk', queries, keys_in, preferred_element_type=jnp.f...  55.3 us
  transfers between devices with their start and end apart: 14, of which 13 were waited for; matrix products, arithmetic and copies ran while one was open for 21% of the time, Pallas kernels for 0%

profile of v1, /device:TPU:0, one launch (start us, length us, event | category | flops | bytes accessed | tf_op | source)
XLA Modules:
  0.0 1410.0 jit_solution(3114345303787107632)
XLA Ops:
  12.9 45.8 %all-gather.3.cloned.1.call-done = bf16[4096,768]{1,0:T(8,128)(2,1)} async-done(((bf16[1024,768]{1,0:T(8,128)(2,1)}), bf16[4096,768]{1,0:T(8,128)(2,1)}) %all-gather.3.cloned.1.call-update) | async-done | bytes 6291472 | tf_op jit(solution)/shard_map/all_gather | solution.py:110
  58.7 6.0 fusion.218
  73.9 35.5 %while.52 = (s32[]{:T(128)}, bf16[8,512,3,64]{1,3,2,0:T(8,128)(2,1)}, f32[8,3,512]{2,1,0:T(4,128)S(1)}, bf16[8,512,3,64]{1,3,2,0:T(8,128)(2,1)}, s32[8,512]{1,0:...) while((s32[]{:T(128)}, ...), condition=%wide.region_5.6_spmd, body=%wide.region_2.5_spmd.sunk | while | flops 211122688 | bytes 11335773 | solution.py:123
  133.2 15.2 %all-to-all-done = bf16[4,1024,192]{1,2,0:T(8,128)(2,1)S(1)} async-done(((bf16[4,1024,192]{1,2,0:T(8,128)(2,1)}), bf16[4,1024,192]{1,2,0:T(8,128)(2,1)S(1)}, u32[]{:S(2)}, u32[]{:S(2)}) %all-to-all-start) | async-done | bytes 1572896 | tf_op jit(solution)/shard_map/all_to_all | solution.py:128
  148.5 4.0 fusion.214
  153.0 39.1 %multiply_convert_fusion.3 = (bf16[1024,3072]{1,0:T(8,128)(2,1)}, f32[1024,3072]{1,0:T(8,128)}, f32[1024,3072]{1,0:T(8,128)}) fusion(f32[3072]{0:T(1024)S(1)} %bitcast.502, bf16[2,768,3072]{2,1,0:T(8,128)(2,1)} %param.31, f32[1024,768]{0,1:T(8,128)S(1)} %get-tuple-element.486, f32[768]{0:T(1024)S(1)} %get-tuple-element.347, ...), kind=kOutput, calls=%fused_computation.148 | convolution fusion | flops 5043388416 | bytes 39348224 | tf_op jit(solution)/shard_map/dot_general | solution.py:144
  192.2 8.6 fusion.215
  203.1 46.5 %all-gather.5.cloned.1.call-done = bf16[4096,768]{0,1:T(8,128)(2,1)} async-done(((bf16[1024,768]{0,1:T(8,128)(2,1)}), bf16[4096,768]{0,1:T(8,128)(2,1)}) %all-gather.5.cloned.1.call-update) | async-done | bytes 6291472 | tf_op jit(solution)/shard_map/all_gather | solution.py:110
  249.6 6.3 fusion.219
  267.4 43.5 %while.53 = (s32[]{:T(128)}, bf16[8,512,3,64]{1,3,2,0:T(8,128)(2,1)}, f32[8,3,512]{2,1,0:T(4,128)S(1)}, bf16[8,512,3,64]{1,3,2,0:T(8,128)(2,1)}, s32[8,512]{1,0:...) while((s32[]{:T(128)}, ...), condition=%wide.region_13.14_spmd, body=%wide.region_10.13_spmd.sunk | while | flops 211122688 | bytes 11335773 | solution.py:123
  330.5 4.4 all-to-all-start.1
  337.4 17.6 %all-to-all-done.1 = bf16[4,1024,192]{1,2,0:T(8,128)(2,1)} async-done(((bf16[4,1024,192]{1,2,0:T(8,128)(2,1)}), bf16[4,1024,192]{1,2,0:T(8,128)(2,1)}, u32[]{:S(2)}, u32[]{:S(2)}) %all-to-all-start.1) | async-done | bytes 1572896 | tf_op jit(solution)/shard_map/all_to_all | solution.py:128
  355.1 3.8 fusion.216
  359.7 39.0 %multiply_convert_fusion.2 = (bf16[1024,3072]{1,0:T(8,128)(2,1)}, f32[1024,3072]{1,0:T(8,128)}, f32[1024,3072]{1,0:T(8,128)}) fusion(f32[3072]{0:T(1024)S(1)} %bitcast.505, bf16[2,768,3072]{2,1,0:T(8,128)(2,1)} %param.31, f32[1024,768]{0,1:T(8,128)S(1)} %get-tuple-element.491, f32[768]{0:T(1024)S(1)} %copy-done.80, f32[768]{0:T(1024)S(1)} %copy-done.57, ...), kind=kOutput, calls=%fused_computation.135 | convolution fusion | flops 5043388416 | bytes 39348224 | tf_op jit(solution)/shard_map/dot_general | solution.py:144
  398.8 8.9 fusion.217
  414.9 18.2 %convert_reduce_fusion = (f32[3072]{0:T(1024)}, bf16[1024,3072]{1,0:T(8,128)(2,1)}) fusion(f32[1024,3072]{1,0:T(8,128)} %get-tuple-element.435, bf16[1024,768]{0,1:T(8,128)(2,1)S(1)} %get-tuple-element.425, bf16[2,3072,768]{2,1,0:T(8,128)(2,1)} %param.33, f32[1024,3072]{1,0:T(8,128)} %get-tuple-element.492, f32[3072]{0:T(1024)S(1)} %bitcast.506), kind=kOutput, calls=%fused_computation.131 | convolution fusion | flops 4885312512 | bytes 37773312 | tf_op jit(solution)/shard_map/rd,fd->rf/dot_general | solution.py:190
  433.1 11.7 multiply_reduce_fusion.2
  455.2 20.0 %all-to-all-done.2 = bf16[1024,4,192]{0,2,1:T(8,128)(2,1)S(1)} async-done(((bf16[1024,4,192]{0,2,1:T(8,128)(2,1)}), bf16[1024,4,192]{0,2,1:T(8,128)(2,1)S(1)}, u32[]{:S(2)}, u32[]{:S(2)}) %all-to-all-start.2) | async-done | bytes 1572896 | tf_op jit(solution)/shard_map/all_to_all | solution.py:213
  483.3 88.3 %while.54 = (s32[]{:T(128)}, bf16[8,512,3,64]{1,3,2,0:T(8,128)(2,1)S(1)}, bf16[8,512,3,64]{1,3,2,0:T(8,128)(2,1)}, bf16[8,512,3,64]{1,3,2,0:T(8,128)(2,1)}, bf16...) while((s32[]{:T(128)}, ...), condition=%wide.region_24.25_spmd, body=%wide.region_22.24_spmd.sunk | while | flops 511146496 | bytes 26125428 | solution.py:215
  587.8 9.4 bitcast_convert_fusion.1
  598.6 4.0 fusion.172
  602.7 11.8 fusion.140
  614.5 41.3 %reduce-scatter.12.cloned.1.call-done = bf16[1024,768]{0,1:T(8,128)(2,1)} async-done(((bf16[4096,768]{0,1:T(8,128)(2,1)}), bf16[1024,768]{0,1:T(8,128)(2,1)}) %reduce-scatter.12.cloned.1.call-update) | async-done | bytes 1572880 | tf_op jit(solution)/shard_map/reduce_scatter | solution.py:238
  655.8 3.9 multiply_reduce_fusion.3
  663.0 18.5 %convert_reduce_fusion.1 = (f32[3072]{0:T(1024)S(1)}, bf16[1024,3072]{1,0:T(8,128)(2,1)}) fusion(f32[1024,3072]{1,0:T(8,128)} %get-tuple-element.437, bf16[1024,768]{0,1:T(8,128)(2,1)} %get-tuple-element.421, bf16[2,3072,768]{2,1,0:T(8,128)(2,1)} %param.33, f32[1024,3072]{1,0:T(8,128)} %get-tuple-element.487, f32[3072]{0:T(1024)S(1)} %bitcast.503), kind=kOutput, calls=%fused_computation.132 | convolution fusion | flops 4885312512 | bytes 37773312 | tf_op jit(solution)/shard_map/rd,fd->rf/dot_general | solution.py:190
  681.6 9.9 multiply_reduce_fusion.4
  697.1 9.1 fusion.141
  706.2 8.4 maximum_bitcast_fusion.1
  714.6 9.3 fusion.139
  723.9 9.8 fusion.138
  733.7 8.3 maximum_bitcast_fusion
  742.1 16.7 %pad_maximum_fusion = bf16[2,2,768,3072]{3,2,1,0:T(8,128)(2,1)} fusion(bf16[1,2,768,3072]{3,2,1,0:T(8,128)(2,1)} %maximum_bitcast_fusion.1, bf16[1,2,768,3072]{3,2,1,0:T(8,128)(2,1)} %maximum_bitcast_fusion), kind=kLoop, calls=%fused_computation.126 | loop fusion | flops 9437184 | bytes 37748736 | tf_op jit(solution)/shard_map/stack | solution.py:269
  762.9 4.3 convolution_convert_fusion.4
  767.3 4.4 all-to-all-start.3
  772.1 9.0 fusion.173
  781.8 10.0 all-to-all-done.3
  791.8 3.8 copy.189
  806.2 102.3 %while.55 = (s32[]{:T(128)}, bf16[8,512,3,64]{1,3,2,0:T(8,128)(2,1)}, bf16[8,512,3,64]{1,3,2,0:T(8,128)(2,1)}, bf16[8,512,3,64]{1,3,2,0:T(8,128)(2,1)}, bf16[8,5...) while((s32[]{:T(128)}, ...), condition=%wide.region_32.33_spmd, body=%wide.region_30.32_spmd.sunk | while | flops 511146496 | bytes 26125428 | solution.py:215
  936.8 8.1 fusion.176
  946.3 5.9 copy.219
  952.2 6.9 reshape.435
  961.6 9.7 bitcast_convert_fusion
  971.3 111.5 %reduce-scatter.18.cloned.1.call-done = bf16[2,2,96,3072]{3,2,1,0:T(8,128)(2,1)} async-done(((bf16[2,2,768,3072]{3,2,1,0:T(8,128)(2,1)}), bf16[2,2,96,3072]{3,2,1,0:T(8,128)(2,1)}) %reduce-scatter.18.cloned.1.call-update) | async-done | bytes 2359312 | tf_op jit(solution)/shard_map/reduce_scatter | solution.py:275
  1085.4 122.8 %all-reduce.3.cloned.1.call-done = (f32[2,8,768]{2,0,1:T(2,128)}, f32[2,3072]{1,0:T(2,128)}) async-done(((f32[2,8,768]{2,0,1:T(2,128)}, f32[2,3072]{1,0:T(2,128)}), (f32[2,8,768]{2,0,1:T(2,128)}, f32[2,3072]{1,0:T(2,128)})) %all-reduce.3.cloned.1.call-update) | async-done | bytes 73744 | tf_op jit(solution)/shard_map/psum | solution.py:293
  1210.9 69.8 %reduce-scatter.22.cloned.1.call-done = bf16[96,1152]{1,0:T(8,128)(2,1)} async-done(((bf16[768,1152]{1,0:T(8,128)(2,1)}), bf16[96,1152]{1,0:T(8,128)(2,1)}) %reduce-scatter.22.cloned.1.call-update) | async-done | bytes 221200
  1285.0 18.6 %reduce-scatter.24.cloned.1.call-done = bf16[192,192]{1,0:T(8,128)(2,1)} async-done(((bf16[768,192]{1,0:T(8,128)(2,1)}), bf16[192,192]{1,0:T(8,128)(2,1)}) %reduce-scatter.24.cloned.1.call-update) | async-done | bytes 73744
  1305.3 59.1 %reduce-scatter.14.cloned.1.call-done = bf16[1024,768]{0,1:T(8,128)(2,1)} async-done(((bf16[4096,768]{0,1:T(8,128)(2,1)}), bf16[1024,768]{0,1:T(8,128)(2,1)}) %reduce-scatter.14.cloned.1.call-update) | async-done | bytes 1572880 | tf_op jit(solution)/shard_map/reduce_scatter | solution.py:238
  1370.2 29.9 %reduce-scatter.20.cloned.1.call-done = bf16[2,2,96,768]{3,2,1,0:T(8,128)(2,1)} async-done(((bf16[2,2,96,3072]{3,2,1,0:T(8,128)(2,1)}), bf16[2,2,96,768]{3,2,1,0:T(8,128)(2,1)}) %reduce-scatter.20.cloned.1.call-update) | async-done | bytes 589840 | tf_op jit(solution)/shard_map/reduce_scatter | solution.py:286
  (603 shorter events, 463.8 us)
Async XLA Ops:
  7.2 51.5 %all-gather.3.cloned.1.call-start = ((), (), s32[]{:S(2)}) async-start(), calls=%async_computation.11 | async-start | bytes 7864320 | tf_op jit(solution)/shard_map/all_gather | solution.py:110
  124.7 23.8 %all-to-all-start = ((bf16[4,1024,192]{1,2,0:T(8,128)(2,1)}), bf16[4,1024,192]{1,2,0:T(8,128)(2,1)S(1)}, u32[]{:S(2)}, u32[]{:S(2)}) async-start(bf16[4,1024,192]{1,2,0:T(8,128)(2,1)} %pad_maximum_fusion.3), calls=%async_computation | async-start | bytes 3145728 | tf_op jit(solution)/shard_map/all_to_all | solution.py:128
  128.4 121.2 %all-gather.5.cloned.1.call-start = ((), (), s32[]{:S(2)}) async-start(), calls=%async_computation.12 | async-start | bytes 7864320 | tf_op jit(solution)/shard_map/all_gather | solution.py:110
  132.0 60.2 %copy-start.55 = (f32[768]{0:T(1024)}, f32[768]{0:T(1024)S(1)}, u32[]{:S(2)}) copy-start(f32[768]{0:T(1024)S(1)} %get-tuple-element.503) | copy-start | bytes 9220
  132.0 60.2 %copy-start.78 = (f32[768]{0:T(1024)}, f32[768]{0:T(1024)S(1)}, u32[]{:S(2)}) copy-start(f32[768]{0:T(1024)S(1)} %get-tuple-element.347) | copy-start | bytes 9220
  132.6 68.7 %copy-start.38 = (f32[768]{0:T(1024)}, f32[768]{0:T(1024)S(1)}, u32[]{:S(2)}) copy-start(f32[768]{0:T(1024)S(1)} %get-tuple-element.505) | copy-start | bytes 9220
  132.6 68.7 %copy-start.59 = (f32[768]{0:T(1024)}, f32[768]{0:T(1024)S(1)}, u32[]{:S(2)}) copy-start(f32[768]{0:T(1024)S(1)} %get-tuple-element.341) | copy-start | bytes 9220
  133.2 19.7 %copy-start.68 = (f32[1,3072]{1,0:T(1,128)}, f32[1,3072]{1,0:T(1,128)S(1)}, u32[]{:S(2)}) copy-start(f32[1,3072]{1,0:T(1,128)S(1)} %get-tuple-element.472) | copy-start | bytes 36868
  148.5 43.7 %slice-start = ((s8[9437184]{0:T(1024)(128)(4,1)}), s8[4194304]{0:T(1024)(128)(4,1)S(1)}, s32[]{:S(2)}) async-start(s8[9437184]{0:T(1024)(128)(4,1)} %bitcast.508), calls=%async_computation.21 | async-start | bytes 8388608
  152.5 39.7 %copy-start.7 = (f32[1024,768]{0,1:T(8,128)}, f32[1024,768]{0,1:T(8,128)S(1)}, u32[]{:S(2)}) copy-start(f32[1024,768]{0,1:T(8,128)S(1)} %get-tuple-element.486) | copy-start | bytes 9437188
  152.5 39.7 %copy-start.45 = (f32[1024]{0:T(1024)}, f32[1024]{0:T(1024)S(1)}, u32[]{:S(2)}) copy-start(f32[1024]{0:T(1024)S(1)} %broadcast_multiply_fusion.3) | copy-start | bytes 12292
  152.9 39.2 %copy-start.47 = (f32[1024]{0:T(1024)}, f32[1024]{0:T(1024)S(1)}, u32[]{:S(2)}) copy-start(f32[1024]{0:T(1024)S(1)} %multiply_reduce_fusion.11) | copy-start | bytes 12292
  152.9 39.2 %copy-start.64 = (f32[1024]{0:T(1024)}, f32[1024]{0:T(1024)S(1)}, u32[]{:S(2)}) copy-start(f32[1024]{0:T(1024)S(1)} %fusion.189) | copy-start | bytes 12292
  153.0 39.2 %slice-start.1 = ((s8[9437184]{0:T(1024)(128)(4,1)}), s8[4194304]{0:T(1024)(128)(4,1)S(1)}, s32[]{:S(2)}) async-start(s8[9437184]{0:T(1024)(128)(4,1)} %bitcast.508), calls=%async_computation.22 | async-start | bytes 8388608
  153.0 39.2 %slice-start.2 = ((s8[9437184]{0:T(1024)(128)(4,1)}), s8[1048576]{0:T(1024)(128)(4,1)S(1)}, s32[]{:S(2)}) async-start(s8[9437184]{0:T(1024)(128)(4,1)} %bitcast.508), calls=%async_computation.23 | async-start | bytes 2097152
  200.9 154.1 %copy-start = (f32[1024,768]{0,1:T(8,128)}, f32[1024,768]{0,1:T(8,128)S(1)}, u32[]{:S(2)}) copy-start(f32[1024,768]{0,1:T(8,128)S(1)} %get-tuple-element.489) | copy-start | bytes 9437188
  330.5 24.5 %copy-start.36 = (f32[1024]{0:T(1024)S(1)}, f32[1024]{0:T(1024)}, u32[]{:S(2)}) copy-start(f32[1024]{0:T(1024)} %copy-done.35) | copy-start | bytes 12292
  330.5 24.5 %copy-start.39 = (f32[768]{0:T(1024)S(1)}, f32[768]{0:T(1024)}, u32[]{:S(2)}) copy-start(f32[768]{0:T(1024)} %copy-done.38) | copy-start | bytes 9220
  330.5 24.5 %copy-start.42 = (f32[1024]{0:T(1024)S(1)}, f32[1024]{0:T(1024)}, u32[]{:S(2)}) copy-start(f32[1024]{0:T(1024)} %copy-done.41) | copy-start | bytes 12292
  330.5 24.5 %copy-start.60 = (f32[768]{0:T(1024)S(1)}, f32[768]{0:T(1024)}, u32[]{:S(2)}) copy-start(f32[768]{0:T(1024)} %copy-done.59) | copy-start | bytes 9220
  330.5 24.6 %copy-start.82 = (f32[768]{0:T(1024)S(1)}, f32[768]{0:T(1024)}, u32[]{:S(2)}) copy-start(f32[768]{0:T(1024)} %get-tuple-element.348) | copy-start | bytes 9220
  330.5 24.5 %all-to-all-start.1 = ((bf16[4,1024,192]{1,2,0:T(8,128)(2,1)}), bf16[4,1024,192]{1,2,0:T(8,128)(2,1)}, u32[]{:S(2)}, u32[]{:S(2)}) async-start(bf16[4,1024,192]{1,2,0:T(8,128)(2,1)} %pad_maximum_fusion.4), calls=%async_computation.1 | async-start | bytes 3145728 | tf_op jit(solution)/shard_map/all_to_all | solution.py:128
  355.0 43.7 %slice-start.3 = ((s8[9437184]{0:T(1024)(128)(4,1)}), s8[4194304]{0:T(1024)(128)(4,1)S(1)}, s32[]{:S(2)}) async-start(s8[9437184]{0:T(1024)(128)(4,1)} %bitcast.510), calls=%async_computation.24 | async-start | bytes 8388608
  358.9 39.8 %copy-start.10 = (f32[1024,768]{0,1:T(8,128)}, f32[1024,768]{0,1:T(8,128)S(1)}, u32[]{:S(2)}) copy-start(f32[1024,768]{0,1:T(8,128)S(1)} %get-tuple-element.491) | copy-start | bytes 9437188
  359.3 39.4 %copy-start.51 = (f32[1024]{0:T(1024)}, f32[1024]{0:T(1024)S(1)}, u32[]{:S(2)}) copy-start(f32[1024]{0:T(1024)S(1)} %multiply_reduce_fusion.9) | copy-start | bytes 12292
  359.7 39.0 %copy-start.81 = (f32[768]{0:T(1024)S(1)}, f32[768]{0:T(1024)}, u32[]{:S(2)}) copy-start(f32[768]{0:T(1024)} %get-tuple-element.342) | copy-start | bytes 9220
  359.7 39.0 %slice-start.4 = ((s8[9437184]{0:T(1024)(128)(4,1)}), s8[4194304]{0:T(1024)(128)(4,1)S(1)}, s32[]{:S(2)}) async-start(s8[9437184]{0:T(1024)(128)(4,1)} %bitcast.510), calls=%async_computation.25 | async-start | bytes 8388608
  359.7 39.0 %slice-start.5 = ((s8[9437184]{0:T(1024)(128)(4,1)}), s8[1048576]{0:T(1024)(128)(4,1)S(1)}, s32[]{:S(2)}) async-start(s8[9437184]{0:T(1024)(128)(4,1)} %bitcast.510), calls=%async_computation.26 | async-start | bytes 2097152
  451.6 23.6 %all-to-all-start.2 = ((bf16[1024,4,192]{0,2,1:T(8,128)(2,1)}), bf16[1024,4,192]{0,2,1:T(8,128)(2,1)S(1)}, u32[]{:S(2)}, u32[]{:S(2)}) async-start(bf16[1024,4,192]{0,2,1:T(8,128)(2,1)} %bitcast.68), calls=%async_computation.2 | async-start | bytes 3145728 | tf_op jit(solution)/shard_map/all_to_all | solution.py:213
  455.2 200.6 %reduce-scatter.12.cloned.1.call-start = ((), (), s32[]{:S(2)}) async-start(), calls=%async_computation.13 | async-start | bytes 7864320 | tf_op jit(solution)/shard_map/reduce_scatter | solution.py:238
  597.3 362.0 %reduce-scatter.16.cloned.1.call-start = ((), (), s32[]{:S(2)}) async-start(), calls=%async_computation.15 | async-start | bytes 2654208 | tf_op jit(solution)/shard_map/reduce_scatter | solution.py:278
  602.7 53.1 %copy-start.1 = (f32[1024,768]{0,1:T(8,128)S(1)}, f32[1024,768]{0,1:T(8,128)}, u32[]{:S(2)}) copy-start(f32[1024,768]{0,1:T(8,128)} %copy-done) | copy-start | bytes 9437188
  602.7 53.1 %copy-start.37 = (f32[1024]{0:T(1024)S(1)}, f32[1024]{0:T(1024)}, u32[]{:S(2)}) copy-start(f32[1024]{0:T(1024)} %copy-done.35) | copy-start | bytes 12292
  602.7 53.1 %copy-start.40 = (f32[768]{0:T(1024)S(1)}, f32[768]{0:T(1024)}, u32[]{:S(2)}) copy-start(f32[768]{0:T(1024)} %copy-done.38) | copy-start | bytes 9220
  602.7 53.1 %copy-start.43 = (f32[1024]{0:T(1024)S(1)}, f32[1024]{0:T(1024)}, u32[]{:S(2)}) copy-start(f32[1024]{0:T(1024)} %copy-done.41) | copy-start | bytes 12292
  614.5 45.2 %copy-start.50 = (f32[1024]{0:T(1024)S(1)}, f32[1024]{0:T(1024)}, u32[]{:S(2)}) copy-start(f32[1024]{0:T(1024)} %copy-done.49) | copy-start | bytes 12292
  663.0 18.5 %copy-start.14 = (f32[1024,768]{0,1:T(8,128)S(1)}, f32[1024,768]{0,1:T(8,128)}, u32[]{:S(2)}) copy-start(f32[1024,768]{0,1:T(8,128)} %copy-done.13) | copy-start | bytes 9437188
  663.0 18.5 %copy-start.46 = (f32[1024]{0:T(1024)S(1)}, f32[1024]{0:T(1024)}, u32[]{:S(2)}) copy-start(f32[1024]{0:T(1024)} %copy-done.45) | copy-start | bytes 12292
  663.0 18.5 %copy-start.56 = (f32[768]{0:T(1024)S(1)}, f32[768]{0:T(1024)}, u32[]{:S(2)}) copy-start(f32[768]{0:T(1024)} %copy-done.55) | copy-start | bytes 9220
  663.0 18.5 %copy-start.65 = (f32[1024]{0:T(1024)S(1)}, f32[1024]{0:T(1024)}, u32[]{:S(2)}) copy-start(f32[1024]{0:T(1024)} %copy-done.64) | copy-start | bytes 12292
  697.1 385.8 %reduce-scatter.18.cloned.1.call-start = ((), (), s32[]{:S(2)}) async-start(), calls=%async_computation.16 | async-start | bytes 21233664 | tf_op jit(solution)/shard_map/reduce_scatter | solution.py:275
  767.3 24.5 %all-to-all-start.3 = ((bf16[1024,4,192]{0,2,1:T(8,128)(2,1)}), bf16[1024,4,192]{0,2,1:T(8,128)(2,1)}, u32[]{:S(2)}, u32[]{:S(2)}) async-start(bf16[1024,4,192]{0,2,1:T(8,128)(2,1)} %bitcast.491), calls=%async_computation.4 | async-start | bytes 3145728 | tf_op jit(solution)/shard_map/all_to_all | solution.py:213
  771.7 436.6 %all-reduce.3.cloned.1.call-start = ((), (), s32[]{:S(2)}) async-start(), calls=%async_computation.20 | async-start | bytes 147456 | tf_op jit(solution)/shard_map/psum | solution.py:293
  936.6 344.1 %reduce-scatter.22.cloned.1.call-start = ((), (), s32[]{:S(2)}) async-start(), calls=%async_computation.18 | async-start | bytes 1990656
  959.2 344.3 %reduce-scatter.24.cloned.1.call-start = ((), (), s32[]{:S(2)}) async-start(), calls=%async_computation.19 | async-start | bytes 491520
  961.5 402.9 %reduce-scatter.14.cloned.1.call-start = ((), (), s32[]{:S(2)}) async-start(), calls=%async_computation.14 | async-start | bytes 7864320 | tf_op jit(solution)/shard_map/reduce_scatter | solution.py:238
  971.3 428.8 %reduce-scatter.20.cloned.1.call-start = ((), (), s32[]{:S(2)}) async-start(), calls=%async_computation.17 | async-start | bytes 2949120 | tf_op jit(solution)/shard_map/reduce_scatter | solution.py:286
  1367.6 34.8 %copy-start.54 = (f32[2,3072]{1,0:T(2,128)S(1)}, f32[2,3072]{1,0:T(2,128)}, u32[]{:S(2)}) copy-start(f32[2,3072]{1,0:T(2,128)} %get-tuple-element.854) | copy-start | bytes 73732
  (58 other events, 289.9 us)
Sparse Core Ops, SparseCore 0:
  9.6 49.0 all-gather.2
  203.2 46.3 all-gather.4
  597.4 58.3 reduce-scatter.11
  697.2 69.0 reduce-scatter.15
  770.4 312.3 reduce-scatter.17
  1090.4 117.7 all-reduce.2
  1212.1 68.5 reduce-scatter.21
  1283.8 19.7 reduce-scatter.23
  1306.1 58.3 reduce-scatter.13
  1367.0 33.0 reduce-scatter.19
